TPU v7x, 256 devices: a 8x8x2 block of a 8x8x16 slice. The times are simulated.
256 devices in a mesh: parts: 2 (over z), seq: 128 (over x, y, core).
Axes of the slice: x: 8, y: 8, z: 2, core: 2. Of those that a mesh axis runs over, the one named last changes fastest.
The devices are a block of a 8x8x16 slice.
Arguments:
- token_ids: int32 [4, 4], P(None, 'parts'), parts along dimension 1, may hold values from 0 to 76031
- lengths: int32 [4], P('parts'), parts along dimension 0, may hold values from 24576 to 32768, as said below
- embed_table: bfloat16 [76032, 5120], P('seq'), may hold values from -6 to 6
- attn_gain: bfloat16 [5120], replicated, may hold values from 0.25 to 1.75
- w_qkv: bfloat16 [5120, 7168], P('seq'), may hold values from -0.3125 to 0.3125
- qkv_bias: float32 [7168], replicated, may hold values from -8 to 8
- cache_keys: bfloat16 [4, 32768, 1024], P('parts', 'seq'), parts along dimension 0, may hold values from -300 to 300
- cache_values: bfloat16 [4, 32768, 1024], P('parts', 'seq'), parts along dimension 0, may hold values from -6 to 6
- w_out: bfloat16 [5120, 5120], P(None, 'seq'), may hold values from -0.078125 to 0.078125
- mlp_gain: bfloat16 [5120], replicated, may hold values from 0.25 to 1.75
- w_gate: bfloat16 [5120, 16384], P(None, 'seq'), may hold values from -0.078125 to 0.078125
- w_up: bfloat16 [5120, 16384], P(None, 'seq'), may hold values from -0.078125 to 0.078125
- w_down: bfloat16 [16384, 5120], P('seq'), may hold values from -0.1875 to 0.1875
Outputs:
- attended: bfloat16 [4, 4, 5120], P(None, 'parts'), parts along dimension 1
- layer_out: bfloat16 [4, 4, 5120], P(None, 'parts', 'seq'), parts along dimension 1
There are 2 independent parts, one for each index of `parts`. A program takes and returns all parts, laid end to end along the dimension named above; an argument that names none is the same for every part. Nothing has to cross between parts.
Inputs may be any that keep to these rules, and one draw needn't show every extreme that they name: Cache positions lengths[b] and later are unused; the first prompt fills the whole cache of 32768 positions.
All inputs are finite; a program needn't handle non-finite values.
Results may differ from a plain program's by a relative error of at most 0.017.
The roundings to bfloat16 on the way count: a program that leaves them out, or rounds other values in their place, can miss the bound.
Values may be sent and summed in bfloat16 or wider, within the bound.
No kernel may reach another device: no remote copies, remote signals or barrier semaphores. Data moves between devices by JAX's collectives and lax.ppermute only.
A program may use at most 128 MiB of HBM per device.

v0:
```python
import math
import jax
import jax.numpy as jnp
from jax import lax
from jax.sharding import Mesh
from jax.sharding import PartitionSpec as P

HEADS = 40
KV_HEADS = 8
HEAD_DIM = 128
SEQ = ("seq_0", "seq_1", "seq_2")
NORM_EPS = 1e-06
ROPE_BASE = 1000000.0
MASKED = -1e30


def gathered_once(array, axis):
    leaves = jax.tree.leaves(array)
    order = sorted(range(len(leaves)), key=lambda k: -leaves[k].size)
    width = (1, *leaves[order[0]].shape)[-1]
    lines = [
        jnp.pad(leaves[k].reshape(-1), (0, -leaves[k].size % width)).reshape(-1, width)
        for k in order
    ]
    both, at, found = (lax.all_gather(jnp.concatenate(lines), axis), 0, {})
    for k, line in zip(order, lines):
        slab = both[:, at : at + len(line)].reshape(len(both), -1)
        found[k] = slab[:, : leaves[k].size].reshape(-1, *leaves[k].shape)
        at += len(line)
    numbers = iter(range(len(leaves)))
    return jax.tree.map(lambda _: found[next(numbers)], array)


def combined_by_axis(array, axes, combine):
    for axis in axes:
        pieces = gathered_once(array, axis)
        array = jax.tree.map(lambda part: part[0], pieces)
        for k in range(1, lax.axis_size(axis)):
            array = combine(array, jax.tree.map(lambda part: part[k], pieces))
    return array


def sum_in_order(parts, axes, order):
    dims = [lax.axis_size(a) for a in axes]
    parts = parts.reshape(*dims, *parts.shape[1:])
    parts = parts.transpose(*order, *range(len(axes), parts.ndim))
    parts = parts.reshape(-1, *parts.shape[len(axes) :])
    for k in order:
        parts = lax.psum_scatter(parts, axes[k], scatter_dimension=0, tiled=True)
    return parts[0]


def cut_along(array, dim, devices):
    before, after = (array.shape[:dim], array.shape[dim + 1 :])
    return jnp.moveaxis(array.reshape(*before, devices, -1, *after), dim, 0)


def scatter_axes(array, axes, order, dim):
    devices = lax.axis_size(axes)
    return sum_in_order(cut_along(array, dim, devices), axes, order)


def rms_normalize(rows, gain):
    mean_square = jnp.mean(rows * rows, axis=-1, keepdims=True)
    return (rows * lax.rsqrt(mean_square + NORM_EPS) * gain.astype(jnp.float32)).astype(
        jnp.bfloat16
    )


def rotate(vectors, positions):
    half_dim = vectors.shape[-1] // 2
    frequency = ROPE_BASE ** (-2.0 * jnp.arange(half_dim, dtype=jnp.float32) / vectors.shape[-1])
    angles = positions.astype(jnp.float32)[..., None, None] * frequency
    cosine = jnp.cos(angles)
    sine_part = jnp.sin(angles)
    widened = vectors.astype(jnp.float32)
    first_half = widened[..., :half_dim]
    second = widened[..., half_dim:]
    joined = jnp.concatenate(
        [first_half * cosine - second * sine_part, second * cosine + first_half * sine_part],
        axis=-1,
    )
    return joined.astype(jnp.bfloat16)


def combine_partials(earlier, latter):
    top_one, total_one, sum_one = earlier
    top_two, total_two, sum_two = latter
    joined_top = jnp.maximum(top_one, top_two)
    scale_one = jnp.exp(top_one - joined_top)
    scale_two = jnp.exp(top_two - joined_top)
    return (
        joined_top,
        total_one * scale_one + total_two * scale_two,
        sum_one * scale_one[..., None] + sum_two * scale_two[..., None],
    )


def body(
    token_ids,
    lengths,
    embed_table,
    attn_gain,
    w_qkv,
    qkv_bias,
    cache_keys,
    cache_values,
    w_out,
    mlp_gain,
    w_gate,
    w_up,
    w_down,
):
    rank = lax.axis_index(SEQ)
    step_count, batch_count = token_ids.shape
    model_width = embed_table.shape[1]
    vocab_rows = embed_table.shape[0]
    query_width = HEADS * HEAD_DIM
    key_width = KV_HEADS * HEAD_DIM
    group_size = HEADS // KV_HEADS
    local_ids = token_ids - rank * vocab_rows
    inside = (local_ids >= 0) & (local_ids < vocab_rows)
    picked = jnp.take(embed_table, jnp.clip(local_ids, 0, vocab_rows - 1), axis=0)
    partial_rows = jnp.where(inside[..., None], picked.astype(jnp.float32), 0.0)
    stream = lax.psum(partial_rows, SEQ)
    normed = rms_normalize(stream, attn_gain).reshape(-1, model_width)
    feature_rows = w_qkv.shape[0]
    normed_local = lax.dynamic_slice_in_dim(normed, rank * feature_rows, feature_rows, 1)
    joint_partial = jnp.dot(normed_local, w_qkv, preferred_element_type=jnp.float32)
    joint_summed = lax.psum(joint_partial, SEQ)
    joint = (joint_summed + qkv_bias).astype(jnp.bfloat16).reshape(step_count, batch_count, -1)
    query_part = joint[..., :query_width].reshape(step_count, batch_count, HEADS, HEAD_DIM)
    key_part = joint[..., query_width : query_width + key_width].reshape(
        step_count, batch_count, KV_HEADS, HEAD_DIM
    )
    value_part = joint[..., query_width + key_width :].reshape(
        step_count, batch_count, KV_HEADS, HEAD_DIM
    )
    positions = lengths[None, :] + jnp.arange(step_count, dtype=jnp.int32)[:, None]
    queries = rotate(query_part, positions)
    new_keys = rotate(key_part, positions)
    grouped = queries.reshape(step_count, batch_count, KV_HEADS, group_size, HEAD_DIM)
    score_scale = 1.0 / math.sqrt(HEAD_DIM)
    local_len = cache_keys.shape[1]
    key_blocks = cache_keys.reshape(batch_count, local_len, KV_HEADS, HEAD_DIM)
    value_blocks = cache_values.reshape(batch_count, local_len, KV_HEADS, HEAD_DIM)
    scores = (
        jnp.einsum("sbkgd,bpkd->bkgsp", grouped, key_blocks, preferred_element_type=jnp.float32)
        * score_scale
    )
    places = rank * local_len + jnp.arange(local_len, dtype=jnp.int32)
    valid = (places[None, :] < lengths[:, None])[:, None, None, None, :]
    masked = jnp.where(valid, scores, MASKED)
    local_top = jnp.max(masked, axis=-1)
    weights = jnp.where(valid, jnp.exp(masked - local_top[..., None]), 0.0)
    local_total = jnp.sum(weights, axis=-1)
    local_sum = jnp.einsum(
        "bkgsp,bpkd->bkgsd",
        weights.astype(jnp.bfloat16),
        value_blocks,
        preferred_element_type=jnp.float32,
    )
    merged_top, merged_total, merged_sum = combined_by_axis(
        (local_top, local_total, local_sum), SEQ, combine_partials
    )
    new_scores = (
        jnp.einsum("sbkgd,tbkd->bkgst", grouped, new_keys, preferred_element_type=jnp.float32)
        * score_scale
    )
    step_index = jnp.arange(step_count, dtype=jnp.int32)
    causal = step_index[:, None] >= step_index[None, :]
    new_masked = jnp.where(causal, new_scores, MASKED)
    final_top = jnp.maximum(merged_top, jnp.max(new_masked, axis=-1))
    rescale = jnp.exp(merged_top - final_top)
    new_weights = jnp.where(causal, jnp.exp(new_masked - final_top[..., None]), 0.0)
    final_total = merged_total * rescale + jnp.sum(new_weights, axis=-1)
    final_sum = merged_sum * rescale[..., None] + jnp.einsum(
        "bkgst,tbkd->bkgsd",
        new_weights.astype(jnp.bfloat16),
        value_part,
        preferred_element_type=jnp.float32,
    )
    attended = jnp.transpose(final_sum / final_total[..., None], (3, 0, 1, 2, 4))
    attended = attended.reshape(step_count, batch_count, query_width).astype(jnp.bfloat16)
    shard_cols = w_out.shape[1]
    projected = jnp.dot(
        attended.reshape(-1, query_width), w_out, preferred_element_type=jnp.float32
    )
    stream_shard = lax.dynamic_slice_in_dim(stream, rank * shard_cols, shard_cols, 2)
    mid_shard = stream_shard + projected.reshape(step_count, batch_count, shard_cols)
    mid_rows = lax.all_gather(mid_shard, SEQ, axis=2, tiled=True)
    normed_mid = rms_normalize(mid_rows, mlp_gain)
    flat_rows = normed_mid.reshape(-1, model_width)
    gate = jnp.dot(flat_rows, w_gate, preferred_element_type=jnp.float32)
    upper = jnp.dot(flat_rows, w_up, preferred_element_type=jnp.float32)
    hidden = (jax.nn.silu(gate) * upper).astype(jnp.bfloat16)
    down_terms = jnp.dot(hidden, w_down, preferred_element_type=jnp.float32).reshape(
        step_count, batch_count, model_width
    )
    summed = scatter_axes(down_terms, SEQ, (2, 1, 0), 2)
    layer_out = (mid_shard + summed).astype(jnp.bfloat16)
    return (attended, layer_out)


def solution(mesh):
    finer = Mesh(
        mesh.devices.reshape(mesh.shape["parts"], 8, 8, 2), ("parts", "seq_0", "seq_1", "seq_2")
    )
    return jax.shard_map(
        body,
        mesh=finer,
        in_specs=(
            P(None, "parts"),
            P("parts"),
            P(SEQ, None),
            P(),
            P(SEQ, None),
            P(),
            P("parts", SEQ, None),
            P("parts", SEQ, None),
            P(None, SEQ),
            P(),
            P(None, SEQ),
            P(None, SEQ),
            P(SEQ, None),
        ),
        out_specs=(P(None, "parts", None), P(None, "parts", SEQ)),
        check_vma=False,
    )
```

profile of v0, /device:TPU:528, one launch (start us, length us, event | category | flops | bytes accessed | tf_op | source)
XLA Modules:
  0.0 717.2 jit_solution(17745230185070453889)
XLA Ops:
  8.3 4.2 gather_fusion
  14.4 1.1 copy-done.3
  15.8 1.1 bitcast_bitcast_fusion
  16.9 195.6 %all-reduce.14.cloned.1.call-done = f32[4,2,5120]{2,1,0:T(2,128)} async-done(((f32[4,2,5120]{2,1,0:T(2,128)}), f32[4,2,5120]{2,1,0:T(2,128)}) %all-reduce.14.cloned.1.call-update) | async-done | bytes 163856 | tf_op jit(solution)/shard_map/psum | solution.py:125
  212.4 1.1 multiply_reduce_fusion.1
  213.5 1.1 multiply_convert_fusion.1
  214.6 1.0 fusion.77
  215.8 181.4 %all-reduce.16.cloned.1.call-done = f32[8,7168]{1,0:T(8,128)} async-done(((f32[8,7168]{1,0:T(8,128)}), f32[8,7168]{1,0:T(8,128)}) %all-reduce.16.cloned.1.call-update) | async-done | bytes 229392 | tf_op jit(solution)/shard_map/psum | solution.py:130
  397.2 1.0 add_convert_fusion
  400.1 1.5 fusion.9
  402.4 38.6 %all-gather.9.cloned.1.call-done = f32[8,326,128]{2,1,0:T(8,128)} async-done(((f32[1,326,128]{2,1,0:T(8,128)}), f32[8,326,128]{2,1,0:T(8,128)}) %all-gather.9.cloned.1.call-update) | async-done | bytes 1335312 | tf_op jit(solution)/shard_map/all_gather | solution.py:25
  442.1 2.0 fusion.39
  446.0 38.5 %all-gather.11.cloned.1.call-done = f32[8,326,128]{2,1,0:T(8,128)} async-done(((f32[1,326,128]{2,1,0:T(8,128)}), f32[8,326,128]{2,1,0:T(8,128)}) %all-gather.11.cloned.1.call-update) | async-done | bytes 1335312 | tf_op jit(solution)/shard_map/all_gather | solution.py:25
  485.6 2.0 fusion.18
  487.6 2.1 all-gather.5
  493.9 56.9 %all_gather.27 = f32[4,2,5120]{0,1,2:T(2,128)} all-gather(f32[4,2,40]{0,1,2:T(2,128)S(1)} %copy.230), channel_id=1, replica_groups=mesh['parts'=2,'seq_0'=8,'seq_1'=8,'seq_2'=2] {'seq_0','seq_1','seq_2'}, dimensions={2}, use_global_device_ids=true | all-gather | bytes 165120 | tf_op jit(solution)/shard_map/all_gather | solution.py:191
  550.8 5.6 copy.233
  556.5 7.0 multiply_reduce_fusion
  564.2 1.9 fusion.8
  566.7 1.1 copy.236
  569.3 30.1 %all-reduce.18.cloned.1.call-done = f32[128,4,2,40]{3,1,2,0:T(4,128)} async-done(((f32[128,4,2,40]{3,1,2,0:T(4,128)}), f32[128,4,2,40]{3,1,2,0:T(4,128)}) %all-reduce.18.cloned.1.call-update) | async-done | bytes 163856
  599.4 1.7 constant_dynamic-slice_fusion.2
  603.0 75.6 %all-reduce.20.cloned.1.call-done = f32[64,4,2,40]{3,1,2,0:T(4,128)} async-done(((f32[64,4,2,40]{3,1,2,0:T(4,128)}), f32[64,4,2,40]{3,1,2,0:T(4,128)}) %all-reduce.20.cloned.1.call-update) | async-done | bytes 81936
  679.4 29.7 %all-reduce.8 = f32[8,4,2,40]{3,1,2,0:T(4,128)S(1)} all-reduce(f32[8,4,2,40]{3,1,2,0:T(4,128)S(1)} %constant_dynamic-slice_fusion.1), channel_id=7, replica_groups=mesh['parts'=2,'seq_0'=8,'seq_1'=8,'seq_2'=2] {'seq_0'}, use_global_device_ids=true, to_apply=%region_10.11.clone | all-reduce | flops 2560 | bytes 20480
  (145 shorter events, 19.3 us)
Async XLA Ops:
  7.2 557.1 %copy-start = (bf16[128,5120]{1,0:T(8,128)(2,1)S(1)}, bf16[128,5120]{1,0:T(8,128)(2,1)}, u32[]{:S(2)}) copy-start(bf16[128,5120]{1,0:T(8,128)(2,1)} %param.25) | copy-start | bytes 3932164
  7.2 6.6 copy-start.7
  7.2 6.6 copy-start.9
  7.2 6.8 copy-start.2
  7.2 205.2 %all-reduce.14.cloned.1.call-start = ((), (), s32[]{:S(2)}) async-start(), calls=%async_computation | async-start | bytes 327680 | tf_op jit(solution)/shard_map/psum | solution.py:125
  13.7 383.5 %all-reduce.16.cloned.1.call-start = ((), (), s32[]{:S(2)}) async-start(), calls=%async_computation.1 | async-start | bytes 458752 | tf_op jit(solution)/shard_map/psum | solution.py:130
  14.3 1.2 copy-start.3
  15.8 198.8 %copy-start.4 = (bf16[40,7168]{1,0:T(8,128)(2,1)S(1)}, bf16[40,7168]{1,0:T(8,128)(2,1)}, u32[]{:S(2)}) copy-start(bf16[40,7168]{1,0:T(8,128)(2,1)} %param.17) | copy-start | bytes 1720324
  16.9 380.3 %copy-start.6 = (f32[7168]{0:T(1024)S(1)}, f32[7168]{0:T(1024)}, u32[]{:S(2)}) copy-start(f32[7168]{0:T(1024)} %param.18) | copy-start | bytes 86020
  215.7 225.3 %all-gather.9.cloned.1.call-start = ((), (), s32[]{:S(2)}) async-start(), calls=%async_computation.2 | async-start | bytes 1511424 | tf_op jit(solution)/shard_map/all_gather | solution.py:25
  402.3 42.6 %copy-start.8 = (bf16[5120]{0:T(1024)(128)(2,1)S(1)}, bf16[5120]{0:T(1024)(128)(2,1)}, u32[]{:S(2)}) copy-start(bf16[5120]{0:T(1024)(128)(2,1)} %param.22) | copy-start | bytes 30724
  402.3 82.2 %all-gather.11.cloned.1.call-start = ((), (), s32[]{:S(2)}) async-start(), calls=%async_computation.3 | async-start | bytes 1511424 | tf_op jit(solution)/shard_map/all_gather | solution.py:25
  444.8 154.6 %all-reduce.18.cloned.1.call-start = ((), (), s32[]{:S(2)}) async-start(), calls=%async_computation.4 | async-start | bytes 1048576
  491.8 1.0 copy-start.10
  492.8 58.0 %copy-start.5 = (bf16[4,2,5120]{2,1,0:T(2,128)(2,1)}, bf16[4,2,5120]{2,1,0:T(2,128)(2,1)S(1)}, u32[]{:S(2)}) copy-start(bf16[4,2,5120]{2,1,0:T(2,128)(2,1)S(1)} %convert_element_type.84) | copy-start | bytes 245764
  556.5 7.5 %copy-start.1 = (bf16[5120,128]{1,0:T(8,128)(2,1)S(1)}, bf16[5120,128]{1,0:T(8,128)(2,1)}, u32[]{:S(2)}) copy-start(bf16[5120,128]{1,0:T(8,128)(2,1)} %param.23) | copy-start | bytes 3932164
  566.5 1.5 copy-start.13
  566.7 34.4 %copy-start.12 = (u32[256]{0:T(256)S(1)}, u32[256]{0:T(256)}, u32[]{:S(2)}) copy-start(u32[256]{0:T(256)} %constant.90) | copy-start | bytes 3076
  566.7 35.0 %copy-start.11 = (u32[256]{0:T(256)S(1)}, u32[256]{0:T(256)}, u32[]{:S(2)}) copy-start(u32[256]{0:T(256)} %constant.94) | copy-start | bytes 3076
  567.9 110.7 %all-reduce.20.cloned.1.call-start = ((), (), s32[]{:S(2)}) async-start(), calls=%async_computation.5 | async-start | bytes 524288
Sparse Core Ops, SparseCore 0:
  13.8 198.6 all-reduce.13
  215.8 181.3 all-reduce.15
  402.5 38.5 all-gather.8
  444.9 39.5 all-gather.10
  568.1 31.3 all-reduce.17
  601.6 77.0 all-reduce.19
where the time goes:
time: 718 us; the launch traced here: 717 us
  waiting for transfers between devices  560 us (78%)
  blocking collectives  88.7 us (12%)
  local copies, waits for them, and re-layouts  25.4 us (4%)
  other arithmetic  19.2 us (3%)
  between operations  16 us (2%)
  matrix products  7.37 us (1%)
    psum x1, waiting for transfers between devices, body(): stream = lax.psum(partial_rows, SEQ)  196 us
    psum x1, waiting for transfers between devices, body(): joint_summed = lax.psum(joint_partial, SEQ)  181 us
    unnamed x8, waiting for transfers between devices  106 us
    all_gather x2, waiting for transfers between devices, gathered_once(): both, at, found = (lax.all_gather(jnp.concatenate(lines), axis), 0, {})  77.1 us
    all_gather x1, blocking collectives, body(): mid_rows = lax.all_gather(mid_shard, SEQ, axis=2, tiled=True)  56.9 us
    unnamed x1, blocking collectives  29.7 us
  transfers between devices with their start and end apart: 6, of which 6 were waited for; matrix products, arithmetic and copies ran while one was open for 1% of the time, Pallas kernels for 0%

commit v1 on v0

--- a/solution.py
+++ b/solution.py
@@ -1,9 +1,11 @@
+import functools
 import math
 import jax
 import jax.numpy as jnp
 from jax import lax
 from jax.sharding import Mesh
 from jax.sharding import PartitionSpec as P
+from jax.lax import psum
 
 HEADS = 40
 KV_HEADS = 8
@@ -12,6 +14,17 @@
 NORM_EPS = 1e-06
 ROPE_BASE = 1000000.0
 MASKED = -1e30
+
+
+def report_the_lane(z, named_axis, device_axis):
+    left_arr = psum(z, named_axis)
+    x_next = psum(left_arr, device_axis)
+    return x_next
+
+
+cover_figure = functools.partial(
+    report_the_lane, named_axis=("seq_1", "seq_2"), device_axis="seq_0"
+)
 
 
 def gathered_once(array, axis):
@@ -127,7 +140,7 @@
     feature_rows = w_qkv.shape[0]
     normed_local = lax.dynamic_slice_in_dim(normed, rank * feature_rows, feature_rows, 1)
     joint_partial = jnp.dot(normed_local, w_qkv, preferred_element_type=jnp.float32)
-    joint_summed = lax.psum(joint_partial, SEQ)
+    joint_summed = cover_figure(joint_partial)
     joint = (joint_summed + qkv_bias).astype(jnp.bfloat16).reshape(step_count, batch_count, -1)
     query_part = joint[..., :query_width].reshape(step_count, batch_count, HEADS, HEAD_DIM)
     key_part = joint[..., query_width : query_width + key_width].reshape(

time: 718 us -> 722 us (level)
    psum x1 -> x2, waiting for transfers between devices: 181 us -> 185 us  [the longest x1 106 us: report_the_lane(): left_arr = psum(z, named_axis)]
    unnamed x8 -> x9, waiting for transfers between devices: 106 us -> 106 us
  transfers between devices with their start and end apart: 6 -> 7, of which waited for: 6 -> 7; matrix products, arithmetic and copies ran while one was open for 1% -> 1% of each run, Pallas kernels for 0% -> 0%
where the time goes in v1:
time: 722 us; the launch traced here: 721 us
  waiting for transfers between devices  564 us (78%)
  blocking collectives  88.7 us (12%)
  local copies, waits for them, and re-layouts  25.4 us (4%)
  other arithmetic  19.2 us (3%)
  between operations  16 us (2%)
  matrix products  7.37 us (1%)
    psum x1, waiting for transfers between devices, body(): stream = lax.psum(partial_rows, SEQ)  196 us
    unnamed x9, waiting for transfers between devices  106 us
    psum x1, waiting for transfers between devices, report_the_lane(): left_arr = psum(z, named_axis)  106 us
    psum x1, waiting for transfers between devices, report_the_lane(): x_next = psum(left_arr, device_axis)  78.9 us
    all_gather x2, waiting for transfers between devices, gathered_once(): both, at, found = (lax.all_gather(jnp.concatenate(lines), axis), 0, {})  77.3 us
    all_gather x1, blocking collectives, body(): mid_rows = lax.all_gather(mid_shard, SEQ, axis=2, tiled=True)  56.9 us
    unnamed x1, blocking collectives  29.7 us
  transfers between devices with their start and end apart: 7, of which 7 were waited for; matrix products, arithmetic and copies ran while one was open for 1% of the time, Pallas kernels for 0%

profile of v1, /device:TPU:528, one launch (start us, length us, event | category | flops | bytes accessed | tf_op | source)
XLA Modules:
  0.0 721.1 jit_solution(14655656197767530887)
XLA Ops:
  8.3 4.2 gather_fusion
  14.2 1.1 copy-done.3
  15.6 1.1 bitcast_bitcast_fusion
  16.7 195.8 %all-reduce.15.cloned.1.call-done = f32[4,2,5120]{2,1,0:T(2,128)} async-done(((f32[4,2,5120]{2,1,0:T(2,128)}), f32[4,2,5120]{2,1,0:T(2,128)}) %all-reduce.15.cloned.1.call-update) | async-done | bytes 163856 | tf_op jit(solution)/shard_map/psum | solution.py:138
  212.5 1.1 multiply_reduce_fusion.1
  213.6 1.1 multiply_convert_fusion.1
  214.7 1.0 fusion.77
  215.9 105.8 %all-reduce.17.cloned.1.call-done = f32[8,7168]{1,0:T(8,128)} async-done(((f32[8,7168]{1,0:T(8,128)}), f32[8,7168]{1,0:T(8,128)}) %all-reduce.17.cloned.1.call-update) | async-done | bytes 229392 | tf_op jit(solution)/shard_map/psum | solution.py:20
  321.9 78.9 %all-reduce.19.cloned.1.call-done = f32[8,7168]{1,0:T(8,128)} async-done(((f32[8,7168]{1,0:T(8,128)}), f32[8,7168]{1,0:T(8,128)}) %all-reduce.19.cloned.1.call-update) | async-done | bytes 229392 | tf_op jit(solution)/shard_map/psum | solution.py:21
  403.7 1.5 fusion.9
  406.0 38.8 %all-gather.9.cloned.1.call-done = f32[8,326,128]{2,1,0:T(8,128)} async-done(((f32[1,326,128]{2,1,0:T(8,128)}), f32[8,326,128]{2,1,0:T(8,128)}) %all-gather.9.cloned.1.call-update) | async-done | bytes 1335312 | tf_op jit(solution)/shard_map/all_gather | solution.py:38
  445.9 2.0 fusion.39
  449.8 38.5 %all-gather.11.cloned.1.call-done = f32[8,326,128]{2,1,0:T(8,128)} async-done(((f32[1,326,128]{2,1,0:T(8,128)}), f32[8,326,128]{2,1,0:T(8,128)}) %all-gather.11.cloned.1.call-update) | async-done | bytes 1335312 | tf_op jit(solution)/shard_map/all_gather | solution.py:38
  489.4 2.0 fusion.18
  491.4 2.1 all-gather.5
  497.7 56.9 %all_gather.27 = f32[4,2,5120]{0,1,2:T(2,128)} all-gather(f32[4,2,40]{0,1,2:T(2,128)S(1)} %copy.230), channel_id=1, replica_groups=mesh['parts'=2,'seq_0'=8,'seq_1'=8,'seq_2'=2] {'seq_0','seq_1','seq_2'}, dimensions={2}, use_global_device_ids=true | all-gather | bytes 165120 | tf_op jit(solution)/shard_map/all_gather | solution.py:204
  554.6 5.6 copy.233
  560.3 7.0 multiply_reduce_fusion
  568.0 1.9 fusion.8
  570.5 1.1 copy.236
  573.1 30.1 %all-reduce.21.cloned.1.call-done = f32[128,4,2,40]{3,1,2,0:T(4,128)} async-done(((f32[128,4,2,40]{3,1,2,0:T(4,128)}), f32[128,4,2,40]{3,1,2,0:T(4,128)}) %all-reduce.21.cloned.1.call-update) | async-done | bytes 163856
  603.2 1.7 constant_dynamic-slice_fusion.2
  606.8 75.7 %all-reduce.23.cloned.1.call-done = f32[64,4,2,40]{3,1,2,0:T(4,128)} async-done(((f32[64,4,2,40]{3,1,2,0:T(4,128)}), f32[64,4,2,40]{3,1,2,0:T(4,128)}) %all-reduce.23.cloned.1.call-update) | async-done | bytes 81936
  683.3 29.7 %all-reduce.8 = f32[8,4,2,40]{3,1,2,0:T(4,128)S(1)} all-reduce(f32[8,4,2,40]{3,1,2,0:T(4,128)S(1)} %constant_dynamic-slice_fusion.1), channel_id=7, replica_groups=mesh['parts'=2,'seq_0'=8,'seq_1'=8,'seq_2'=2] {'seq_0'}, use_global_device_ids=true, to_apply=%region_11.12.clone | all-reduce | flops 2560 | bytes 20480
  (148 shorter events, 20.4 us)
Async XLA Ops:
  7.2 560.9 %copy-start = (bf16[128,5120]{1,0:T(8,128)(2,1)S(1)}, bf16[128,5120]{1,0:T(8,128)(2,1)}, u32[]{:S(2)}) copy-start(bf16[128,5120]{1,0:T(8,128)(2,1)} %param.25) | copy-start | bytes 3932164
  7.2 6.5 copy-start.7
  7.2 6.6 copy-start.9
  7.2 6.6 copy-start.2
  7.2 205.2 %all-reduce.15.cloned.1.call-start = ((), (), s32[]{:S(2)}) async-start(), calls=%async_computation | async-start | bytes 327680 | tf_op jit(solution)/shard_map/psum | solution.py:138
  13.7 308.0 %all-reduce.17.cloned.1.call-start = ((), (), s32[]{:S(2)}) async-start(), calls=%async_computation.1 | async-start | bytes 458752 | tf_op jit(solution)/shard_map/psum | solution.py:20
  14.1 1.2 copy-start.3
  15.6 199.0 %copy-start.4 = (bf16[40,7168]{1,0:T(8,128)(2,1)S(1)}, bf16[40,7168]{1,0:T(8,128)(2,1)}, u32[]{:S(2)}) copy-start(bf16[40,7168]{1,0:T(8,128)(2,1)} %param.17) | copy-start | bytes 1720324
  16.7 384.1 %copy-start.6 = (f32[7168]{0:T(1024)S(1)}, f32[7168]{0:T(1024)}, u32[]{:S(2)}) copy-start(f32[7168]{0:T(1024)} %param.18) | copy-start | bytes 86020
  215.7 185.1 %all-reduce.19.cloned.1.call-start = ((), (), s32[]{:S(2)}) async-start(), calls=%async_computation.2 | async-start | bytes 458752 | tf_op jit(solution)/shard_map/psum | solution.py:21
  321.7 123.1 %all-gather.9.cloned.1.call-start = ((), (), s32[]{:S(2)}) async-start(), calls=%async_computation.3 | async-start | bytes 1511424 | tf_op jit(solution)/shard_map/all_gather | solution.py:38
  405.9 42.8 %copy-start.8 = (bf16[5120]{0:T(1024)(128)(2,1)S(1)}, bf16[5120]{0:T(1024)(128)(2,1)}, u32[]{:S(2)}) copy-start(bf16[5120]{0:T(1024)(128)(2,1)} %param.22) | copy-start | bytes 30724
  405.9 82.4 %all-gather.11.cloned.1.call-start = ((), (), s32[]{:S(2)}) async-start(), calls=%async_computation.4 | async-start | bytes 1511424 | tf_op jit(solution)/shard_map/all_gather | solution.py:38
  448.6 154.6 %all-reduce.21.cloned.1.call-start = ((), (), s32[]{:S(2)}) async-start(), calls=%async_computation.5 | async-start | bytes 1048576
  495.6 1.0 copy-start.10
  496.6 58.0 %copy-start.5 = (bf16[4,2,5120]{2,1,0:T(2,128)(2,1)}, bf16[4,2,5120]{2,1,0:T(2,128)(2,1)S(1)}, u32[]{:S(2)}) copy-start(bf16[4,2,5120]{2,1,0:T(2,128)(2,1)S(1)} %convert_element_type.84) | copy-start | bytes 245764
  560.3 7.5 %copy-start.1 = (bf16[5120,128]{1,0:T(8,128)(2,1)S(1)}, bf16[5120,128]{1,0:T(8,128)(2,1)}, u32[]{:S(2)}) copy-start(bf16[5120,128]{1,0:T(8,128)(2,1)} %param.23) | copy-start | bytes 3932164
  570.3 1.5 copy-start.13
  570.5 34.4 %copy-start.12 = (u32[256]{0:T(256)S(1)}, u32[256]{0:T(256)}, u32[]{:S(2)}) copy-start(u32[256]{0:T(256)} %constant.90) | copy-start | bytes 3076
  570.5 35.0 %copy-start.11 = (u32[256]{0:T(256)S(1)}, u32[256]{0:T(256)}, u32[]{:S(2)}) copy-start(u32[256]{0:T(256)} %constant.94) | copy-start | bytes 3076
  571.7 110.8 %all-reduce.23.cloned.1.call-start = ((), (), s32[]{:S(2)}) async-start(), calls=%async_computation.6 | async-start | bytes 524288
Sparse Core Ops, SparseCore 0:
  13.8 198.6 all-reduce.14
  215.8 105.8 all-reduce.16
  324.1 76.6 all-reduce.18
  406.0 38.7 all-gather.8
  448.7 39.5 all-gather.10
  571.9 31.3 all-reduce.20
  605.5 76.9 all-reduce.22
